TPU v7x, 128 devices: a whole 4x4x4 slice. The times are simulated.
128 devices in a mesh: ya: 32 (over z, y, core), zb: 4 (over x).
Axes of the slice: x: 4, y: 4, z: 4, core: 2. Of those that a mesh axis runs over, the one named last changes fastest.
Arguments:
- source: float32 [512, 512, 512], P(None, 'ya', 'zb'), may hold values from -6 to 6
- symbol_x: float32 [512], replicated, may hold values from 0.3 to 3
- symbol_y: float32 [512], replicated, may hold values from 0.3 to 3
- symbol_z: float32 [512], replicated, may hold values from 0.3 to 3
Outputs:
- modes: float32 [512, 512, 512], P('ya', 'zb')
All inputs are finite; a program needn't handle non-finite values.
Results may differ from a plain program's by a relative error of at most 0.000071.
Values sent between devices are 32-bit elements; how exact they have to be, the bound alone decides.
A program may use at most 64 MiB of HBM per device.

v0:
```python
import functools

import jax
import jax.numpy as jnp
import ml_dtypes
import numpy as np
from jax import lax
from jax.experimental import pallas as pl
from jax.experimental.pallas import tpu as pltpu
from jax.sharding import PartitionSpec as P

MESH = pl.DeviceIdType.MESH


def scoped(f):
    def g(*args):
        with jax.named_scope(f.__name__):
            return f(*args)

    return g

N = 512
ORDER = [i * 7 % 31 + 1 for i in range(31)]
EARLY = 2
YPARTS = ((1, 3), (2, 0))
AHEAD = 5
LAG = 2


def table():
    rank = np.arange(1, N + 1)
    angle = np.pi * (rank[:, None] * rank[None, :] % (2 * N + 2)) / (N + 1)
    return np.sqrt(2.0 / (N + 1)) * np.sin(angle)


def halves(h):
    high = h.astype(ml_dtypes.bfloat16)
    return high, (h - high.astype(np.float64)).astype(ml_dtypes.bfloat16)


def split(v):
    high = v.astype(jnp.bfloat16)
    return high, (v - high.astype(jnp.float32)).astype(jnp.bfloat16)


def dot(a, b):
    return jnp.dot(a, b, preferred_element_type=jnp.float32)


def kernel(
    src, h1_hbm, hh_hbm, hl_hbm, sx_hbm, sy_hbm, sz_hbm, out,
    xin, xh, xl, h1, hh, hl, a_early, a_out, a_in, b_out, b_in, ycol, sx, sy, sz,
    load_sem, table_sem, a_send, a_recv, a_own, b_send, b_recv,
):
    ya, zb = lax.axis_index("ya"), lax.axis_index("zb")

    def load(y):
        return pltpu.make_async_copy(src.at[:, y, 0, :], xin.at[y], load_sem.at[y])

    tables = [
        pltpu.make_async_copy(s, d, table_sem.at[k])
        for k, (s, d) in enumerate(
            ((h1_hbm, h1), (hh_hbm, hh), (hl_hbm, hl), (sx_hbm, sx), (sy_hbm, sy), (sz_hbm, sz))
        )
    ]
    tables[0].start()
    for y in range(16):
        load(y).start()

    def peer_a(o):
        return ya ^ o

    barrier = pltpu.get_barrier_semaphore()
    for o in ORDER:
        pl.semaphore_signal(barrier, inc=1, device_id=(peer_a(o), zb), device_id_type=MESH)
    for d in (1, 3, 2):
        pl.semaphore_signal(barrier, inc=1, device_id=(ya, (zb + d) & 3), device_id_type=MESH)
    for t in tables[1:]:
        t.start()

    def a_slot(c, who):
        return a_in.at[pl.ds(pl.multiple_of(c * 512 + who * 16, 16), 16)]

    def a_source(c, who):
        if isinstance(c, int) and c < EARLY:
            return a_early.at[pl.ds(pl.multiple_of(c * 512 + who * 16, 16), 16)]
        return a_out.at[pl.ds(pl.multiple_of(who * 256 + c * 16, 16), 16)]

    def a_all(c):
        return a_in.at[pl.ds(pl.multiple_of(c * 512, 512), 31 * 16)]

    @scoped
    def send_a(c):
        pltpu.make_async_copy(a_source(c, ya), a_slot(c, ya), a_own.at[c]).start()
        for o in ORDER:
            peer = peer_a(o)
            pltpu.make_async_remote_copy(
                src_ref=a_source(c, peer),
                dst_ref=a_slot(c, ya),
                send_sem=a_send.at[c],
                recv_sem=a_recv.at[c],
                device_id=(peer, zb),
                device_id_type=MESH,
            ).start()

    @scoped
    def wait_a(c):
        pltpu.make_async_copy(a_slot(c, ya), a_slot(c, ya), a_own.at[c]).wait()
        pltpu.make_async_copy(a_all(c), a_all(c), a_recv.at[c]).wait()

    @scoped
    def transform_y(c):
        bh, bl = split(a_in[pl.ds(pl.multiple_of(c * 512, 512), 512), :])
        rhs = jnp.concatenate([bh, bh, bl], axis=0)
        for ds in YPARTS:
            blocks = [(zb + d) & 3 for d in ds]
            rows = [pl.ds(pl.multiple_of(b * 128, 128), 128) for b in blocks]
            high = jnp.concatenate([hh[r, :] for r in rows], axis=0)
            low = jnp.concatenate([hl[r, :] for r in rows], axis=0)
            r = dot(jnp.concatenate([high, low, high], axis=1), rhs)
            for i, (d, b) in enumerate(zip(ds, blocks)):
                target = b_out if d else b_in
                target[c * 4 + b] = r[128 * i : 128 * i + 128, :]
                if d:
                    pltpu.make_async_remote_copy(
                        src_ref=b_out.at[c * 4 + b],
                        dst_ref=b_in.at[c * 4 + zb],
                        send_sem=b_send.at[c],
                        recv_sem=b_recv.at[c],
                        device_id=(ya, b),
                        device_id_type=MESH,
                    ).start()

    def b_all(ref, c):
        return ref.at[pl.ds(c * 4, 3)]

    @scoped
    def wait_b(c):
        pltpu.make_async_copy(b_all(b_in, c), b_all(b_in, c), b_recv.at[c]).wait()

    @scoped
    def transform_z(c):
        ah, al = split(jnp.concatenate([b_in[c * 4 + b] for b in range(4)], axis=1))
        lhs = jnp.concatenate([ah, ah, al], axis=1)
        column = ycol[...] + sx[ya * 16 + c]
        for k in range(2):
            cols = slice(256 * k, 256 * k + 256)
            rhs = jnp.concatenate([hh[:, cols], hl[:, cols], hh[:, cols]], axis=0)
            r = dot(lhs, rhs)
            for j in range(2):
                n = 2 * k + j
                scale = lax.rsqrt(column + sz[pl.ds(n, 1), :])
                out[c, :, 128 * n : 128 * n + 128] = r[:, 128 * j : 128 * j + 128] * scale

    rows = 32 * EARLY
    with jax.named_scope("early"):
        for g in range(4):
            bhs, bls = [], []
            for y in range(4 * g, 4 * g + 4):
                load(y).wait()
                high, low = split(xin[y])
                xh[y] = high
                xl[y] = low
                bhs.append(high)
                bls.append(low)
            if g == 0:
                tables[0].wait()
            bh, bl = jnp.concatenate(bhs, axis=1), jnp.concatenate(bls, axis=1)
            both = dot(h1[...], bh)
            r = both[:rows] + (both[rows:] + dot(h1[pl.ds(0, rows), :], bl))
            for k in range(4):
                a_early[pl.ds(4 * g + k, rows, stride=16), :] = r[:, 128 * k : 128 * k + 128]
    with jax.named_scope("barrier_wait"):
        pl.semaphore_wait(barrier, 34)
    for c in range(EARLY):
        send_a(c)
    for t in tables[1:]:
        t.wait()
    with jax.named_scope("rest"):

        @pl.loop(0, 8)
        def _(g):
            bh = jnp.concatenate([xh[2 * g], xh[2 * g + 1]], axis=1)
            bl = jnp.concatenate([xl[2 * g], xl[2 * g + 1]], axis=1)
            rhs = jnp.concatenate([bh, bh, bl], axis=0)
            r = dot(jnp.concatenate([hh[...], hl[...], hh[...]], axis=1), rhs)
            for k in range(2):
                a_out[pl.ds(2 * g + k, 512, stride=16), :] = r[:, 128 * k : 128 * k + 128]

    @pl.loop(EARLY, AHEAD)
    def _(c):
        send_a(c)

    ycol[...] = jnp.transpose(jnp.broadcast_to(sy[pl.ds(zb, 1), :], (128, 128)))

    @pl.loop(0, 16)
    def _(c):
        wait_a(c)
        transform_y(c)

        @pl.when(c + AHEAD < 16)
        def _():
            send_a(c + AHEAD)

        @pl.when(c >= LAG)
        def _():
            wait_b(c - LAG)
            transform_z(c - LAG)

    @pl.loop(16 - LAG, 16)
    def _(c):
        wait_b(c)
        transform_z(c)

    with jax.named_scope("drain"):

        @pl.loop(0, 16)
        def _(c):
            pltpu.make_async_copy(a_all(c), a_all(c), a_send.at[c]).wait()
            pltpu.make_async_copy(b_all(b_out, c), b_all(b_out, c), b_send.at[c]).wait()


def body(source, symbol_x, symbol_y, symbol_z):
    high, low = halves(table())
    order = np.array([a * 16 + c for c in range(EARLY) for a in range(32)])
    stacked = np.concatenate([high[order], low[order]])
    any_space = pl.BlockSpec(memory_space=pl.ANY)
    f32, bf16 = jnp.float32, jnp.bfloat16
    return pl.pallas_call(
        kernel,
        out_shape=pltpu.VMEM((16, 128, 512), f32),
        in_specs=[any_space] * 7,
        out_specs=pl.BlockSpec(memory_space=pltpu.VMEM),
        scratch_shapes=[
            pltpu.VMEM((16, 512, 128), f32),
            pltpu.VMEM((16, 512, 128), bf16),
            pltpu.VMEM((16, 512, 128), bf16),
            pltpu.VMEM(stacked.shape, bf16),
            pltpu.VMEM((512, 512), bf16),
            pltpu.VMEM((512, 512), bf16),
            pltpu.VMEM((len(order) * 16, 128), f32),
            pltpu.VMEM((8192, 128), f32),
            pltpu.VMEM((8192, 128), f32),
            pltpu.VMEM((64, 128, 128), f32),
            pltpu.VMEM((64, 128, 128), f32),
            pltpu.VMEM((128, 128), f32),
            pltpu.SMEM((512,), f32),
            pltpu.VMEM((4, 128), f32),
            pltpu.VMEM((4, 128), f32),
            pltpu.SemaphoreType.DMA((16,)),
            pltpu.SemaphoreType.DMA((6,)),
            pltpu.SemaphoreType.DMA((16,)),
            pltpu.SemaphoreType.DMA((16,)),
            pltpu.SemaphoreType.DMA((16,)),
            pltpu.SemaphoreType.DMA((16,)),
            pltpu.SemaphoreType.DMA((16,)),
        ],
        compiler_params=pltpu.CompilerParams(
            collective_id=0, has_side_effects=True, vmem_limit_bytes=67043328 - 4 * 1024 * 1024 - 65536
        ),
    )(
        source.reshape(512, 16, 1, 128),
        jnp.asarray(stacked),
        jnp.asarray(high),
        jnp.asarray(low),
        symbol_x,
        symbol_y.reshape(4, 128),
        symbol_z.reshape(4, 128),
    )


def solution(mesh):
    placed = (P(None, "ya", "zb"), P(), P(), P())
    return jax.shard_map(
        body, mesh=mesh, in_specs=placed, out_specs=P("ya", "zb", None), check_vma=False
    )
```

profile of v0, /device:TPU:1, one launch (start us, length us, event | category | flops | bytes accessed | tf_op | source)
XLA Modules:
  0.0 67.4 jit_solution(15206220546057608927)
XLA Ops:
  0.0 65.4 %shard_map.73 = f32[16,128,512]{2,1,0:T(8,128)S(1)} custom-call(f32[512,16,1,128]{3,2,1,0:T(1,128)} %bitcast.3, bf16[128,512]{1,0:T(8,128)(2,1)} %constant.6.clone.h1_hbm, bf16[512,512]{1,0:T(8,128)(2,1)} %constant.7.clone.hh_hbm, bf16[512,512]{1,0:T(8,128)(2,1)} %constant.8.clone.hl_hbm, f32[512]{0:T(512)} %sx_hbm.1, f32[4,128]{1,0:T(4,128)} %bitcast.4, ...), custom_call_target="tpu_custom_call" | custom-call | tf_op jit(solution)/shard_map/pallas_call | solution.py:229
  65.4 2.0 %copy.9 = f32[16,128,512]{2,1,0:T(8,128)} copy(f32[16,128,512]{2,1,0:T(8,128)S(1)} %shard_map.73) | data formatting | bytes 8388608
where the time goes:
time: 67.5 us; the launch traced here: 67.4 us
  Pallas kernels  65.4 us (97%)
  local copies, waits for them, and re-layouts  2.02 us (3%)
    pallas_call x1, Pallas kernels, body(): pl.pallas_call(kernel, out_shape=pltpu.VMEM((16, 128, 512), f32), in_spec...  65.4 us
    unnamed x1, local copies, waits for them, and re-layouts  2.02 us

commit v1 on v0

--- a/solution.py
+++ b/solution.py
@@ -20,10 +20,10 @@
     return g
 
 N = 512
-ORDER = [i * 7 % 31 + 1 for i in range(31)]
+FAR = (10, 11, 14, 9, 6, 5, 7, 13, 15, 8, 2, 1, 4, 3, 12)
 EARLY = 2
 YPARTS = ((1, 3), (2, 0))
-AHEAD = 5
+AHEAD = 3
 LAG = 2
 
 
@@ -50,12 +50,12 @@
 def kernel(
     src, h1_hbm, hh_hbm, hl_hbm, sx_hbm, sy_hbm, sz_hbm, out,
     xin, xh, xl, h1, hh, hl, a_early, a_out, a_in, b_out, b_in, ycol, sx, sy, sz,
-    load_sem, table_sem, a_send, a_recv, a_own, b_send, b_recv,
+    load_sem, table_sem, a_send, a_recv, b_send, b_recv,
 ):
     ya, zb = lax.axis_index("ya"), lax.axis_index("zb")
 
     def load(y):
-        return pltpu.make_async_copy(src.at[:, y, 0, :], xin.at[y], load_sem.at[y])
+        return pltpu.make_async_copy(src.at[:, y, 0, :], xin.at[y], load_sem.at[y // 4])
 
     tables = [
         pltpu.make_async_copy(s, d, table_sem.at[k])
@@ -64,17 +64,17 @@
         )
     ]
     tables[0].start()
+
+    chip, core = ya >> 1, ya & 1
+    peers = [(chip ^ p) * 2 + 1 for p in FAR] + [chip * 2 + 1 - core] + [(chip ^ p) * 2 for p in FAR]
+
+    barrier = pltpu.get_barrier_semaphore()
+    for peer in peers:
+        pl.semaphore_signal(barrier, inc=1, device_id=(peer, zb), device_id_type=MESH)
+    for d in (1, 3, 2):
+        pl.semaphore_signal(barrier, inc=1, device_id=(ya, (zb + d) & 3), device_id_type=MESH)
     for y in range(16):
         load(y).start()
-
-    def peer_a(o):
-        return ya ^ o
-
-    barrier = pltpu.get_barrier_semaphore()
-    for o in ORDER:
-        pl.semaphore_signal(barrier, inc=1, device_id=(peer_a(o), zb), device_id_type=MESH)
-    for d in (1, 3, 2):
-        pl.semaphore_signal(barrier, inc=1, device_id=(ya, (zb + d) & 3), device_id_type=MESH)
     for t in tables[1:]:
         t.start()
 
@@ -86,18 +86,14 @@
             return a_early.at[pl.ds(pl.multiple_of(c * 512 + who * 16, 16), 16)]
         return a_out.at[pl.ds(pl.multiple_of(who * 256 + c * 16, 16), 16)]
 
-    def a_all(c):
-        return a_in.at[pl.ds(pl.multiple_of(c * 512, 512), 31 * 16)]
-
     @scoped
     def send_a(c):
-        pltpu.make_async_copy(a_source(c, ya), a_slot(c, ya), a_own.at[c]).start()
-        for o in ORDER:
-            peer = peer_a(o)
+        pltpu.make_async_copy(a_source(c, ya), a_slot(c, ya), a_recv.at[c]).start()
+        for peer in peers:
             pltpu.make_async_remote_copy(
                 src_ref=a_source(c, peer),
                 dst_ref=a_slot(c, ya),
-                send_sem=a_send.at[c],
+                send_sem=a_send,
                 recv_sem=a_recv.at[c],
                 device_id=(peer, zb),
                 device_id_type=MESH,
@@ -105,8 +101,8 @@
 
     @scoped
     def wait_a(c):
-        pltpu.make_async_copy(a_slot(c, ya), a_slot(c, ya), a_own.at[c]).wait()
-        pltpu.make_async_copy(a_all(c), a_all(c), a_recv.at[c]).wait()
+        slots = a_in.at[pl.ds(pl.multiple_of(c * 512, 512), 512)]
+        pltpu.make_async_copy(slots, slots, a_recv.at[c]).wait()
 
     @scoped
     def transform_y(c):
@@ -125,18 +121,16 @@
                     pltpu.make_async_remote_copy(
                         src_ref=b_out.at[c * 4 + b],
                         dst_ref=b_in.at[c * 4 + zb],
-                        send_sem=b_send.at[c],
+                        send_sem=b_send,
                         recv_sem=b_recv.at[c],
                         device_id=(ya, b),
                         device_id_type=MESH,
                     ).start()
 
-    def b_all(ref, c):
-        return ref.at[pl.ds(c * 4, 3)]
-
     @scoped
     def wait_b(c):
-        pltpu.make_async_copy(b_all(b_in, c), b_all(b_in, c), b_recv.at[c]).wait()
+        slots = b_in.at[pl.ds(c * 4, 3)]
+        pltpu.make_async_copy(slots, slots, b_recv.at[c]).wait()
 
     @scoped
     def transform_z(c):
@@ -156,15 +150,18 @@
     with jax.named_scope("early"):
         for g in range(4):
             bhs, bls = [], []
+            landed = xin.at[pl.ds(4 * g, 4)]
+            with jax.named_scope(f'ld{g}'):
+                pltpu.make_async_copy(landed, landed, load_sem.at[g]).wait()
             for y in range(4 * g, 4 * g + 4):
-                load(y).wait()
                 high, low = split(xin[y])
                 xh[y] = high
                 xl[y] = low
                 bhs.append(high)
                 bls.append(low)
             if g == 0:
-                tables[0].wait()
+                with jax.named_scope('tab'):
+                    tables[0].wait()
             bh, bl = jnp.concatenate(bhs, axis=1), jnp.concatenate(bls, axis=1)
             both = dot(h1[...], bh)
             r = both[:rows] + (both[rows:] + dot(h1[pl.ds(0, rows), :], bl))
@@ -178,14 +175,16 @@
         t.wait()
     with jax.named_scope("rest"):
 
-        @pl.loop(0, 8)
+        @pl.loop(0, 8, unroll=4)
         def _(g):
-            bh = jnp.concatenate([xh[2 * g], xh[2 * g + 1]], axis=1)
-            bl = jnp.concatenate([xl[2 * g], xl[2 * g + 1]], axis=1)
+            bh = jnp.concatenate([xh[2 * g + k] for k in range(2)], axis=1)
+            bl = jnp.concatenate([xl[2 * g + k] for k in range(2)], axis=1)
             rhs = jnp.concatenate([bh, bh, bl], axis=0)
-            r = dot(jnp.concatenate([hh[...], hl[...], hh[...]], axis=1), rhs)
-            for k in range(2):
-                a_out[pl.ds(2 * g + k, 512, stride=16), :] = r[:, 128 * k : 128 * k + 128]
+            for p in range(1):
+                rows = slice(512 * p, 512 * p + 512)
+                r = dot(jnp.concatenate([hh[rows, :], hl[rows, :], hh[rows, :]], axis=1), rhs)
+                for k in range(2):
+                    a_out[pl.ds(512 * 16 * p + 2 * g + k, 512, stride=16), :] = r[:, 128 * k : 128 * k + 128]
 
     @pl.loop(EARLY, AHEAD)
     def _(c):
@@ -214,10 +213,10 @@
 
     with jax.named_scope("drain"):
 
-        @pl.loop(0, 16)
-        def _(c):
-            pltpu.make_async_copy(a_all(c), a_all(c), a_send.at[c]).wait()
-            pltpu.make_async_copy(b_all(b_out, c), b_all(b_out, c), b_send.at[c]).wait()
+        sent = a_in.at[pl.ds(0, 16 * 31 * 16)]
+        pltpu.make_async_copy(sent, sent, a_send).wait()
+        sent = b_out.at[pl.ds(0, 16 * 3)]
+        pltpu.make_async_copy(sent, sent, b_send).wait()
 
 
 def body(source, symbol_x, symbol_y, symbol_z):
@@ -247,12 +246,11 @@
             pltpu.SMEM((512,), f32),
             pltpu.VMEM((4, 128), f32),
             pltpu.VMEM((4, 128), f32),
+            pltpu.SemaphoreType.DMA((4,)),
+            pltpu.SemaphoreType.DMA((6,)),
+            pltpu.SemaphoreType.DMA,
             pltpu.SemaphoreType.DMA((16,)),
-            pltpu.SemaphoreType.DMA((6,)),
-            pltpu.SemaphoreType.DMA((16,)),
-            pltpu.SemaphoreType.DMA((16,)),
-            pltpu.SemaphoreType.DMA((16,)),
-            pltpu.SemaphoreType.DMA((16,)),
+            pltpu.SemaphoreType.DMA,
             pltpu.SemaphoreType.DMA((16,)),
         ],
         compiler_params=pltpu.CompilerParams(

time: 67.5 us -> 65.3 us (0.967)
  Pallas kernels: 65.4 us -> 63 us
    pallas_call x1, Pallas kernels: 65.4 us -> 63 us  [body(): pl.pallas_call(kernel, out_shape=pltpu.VMEM((16, 128, 512), f32), in_spec...]
where the time goes in v1:
time: 65.3 us; the launch traced here: 65.1 us
  Pallas kernels  63 us (96%)
  local copies, waits for them, and re-layouts  2.02 us (3%)
    pallas_call x1, Pallas kernels, body(): pl.pallas_call(kernel, out_shape=pltpu.VMEM((16, 128, 512), f32), in_spec...  63 us
    unnamed x1, local copies, waits for them, and re-layouts  2.02 us

profile of v1, /device:TPU:1, one launch (start us, length us, event | category | flops | bytes accessed | tf_op | source)
XLA Modules:
  0.0 65.1 jit_solution(9236626218004376561)
XLA Ops:
  0.0 63.0 %shard_map.73 = f32[16,128,512]{2,1,0:T(8,128)S(1)} custom-call(f32[512,16,1,128]{3,2,1,0:T(1,128)} %bitcast.3, bf16[128,512]{1,0:T(8,128)(2,1)} %constant.6.clone.h1_hbm, bf16[512,512]{1,0:T(8,128)(2,1)} %constant.7.clone.hh_hbm, bf16[512,512]{1,0:T(8,128)(2,1)} %constant.8.clone.hl_hbm, f32[512]{0:T(512)} %sx_hbm.1, f32[4,128]{1,0:T(4,128)} %bitcast.4, ...), custom_call_target="tpu_custom_call" | custom-call | tf_op jit(solution)/shard_map/pallas_call | solution.py:228
  63.0 2.0 %copy.9 = f32[16,128,512]{2,1,0:T(8,128)} copy(f32[16,128,512]{2,1,0:T(8,128)S(1)} %shard_map.73) | data formatting | bytes 8388608

commit v2 on v1

--- a/solution.py
+++ b/solution.py
@@ -25,6 +25,7 @@
 YPARTS = ((1, 3), (2, 0))
 AHEAD = 3
 LAG = 2
+GROUPS = ((0, 4), (4, 4), (8, 4), (12, 4))
 
 
 def table():
@@ -55,7 +56,8 @@
     ya, zb = lax.axis_index("ya"), lax.axis_index("zb")
 
     def load(y):
-        return pltpu.make_async_copy(src.at[:, y, 0, :], xin.at[y], load_sem.at[y // 4])
+        group = max(g for g in range(len(GROUPS)) if GROUPS[g][0] <= y)
+        return pltpu.make_async_copy(src.at[:, y, 0, :], xin.at[y], load_sem.at[group])
 
     tables = [
         pltpu.make_async_copy(s, d, table_sem.at[k])
@@ -64,19 +66,23 @@
         )
     ]
     tables[0].start()
-
-    chip, core = ya >> 1, ya & 1
-    peers = [(chip ^ p) * 2 + 1 for p in FAR] + [chip * 2 + 1 - core] + [(chip ^ p) * 2 for p in FAR]
+    for y in range(4):
+        load(y).start()
+
+    z0, y0 = ya >> 3, (ya >> 1) & 3
+    peers = [z * 8 + y * 2 + k for k in (1, 0) for z in (0, 1, 3, 2) for y in (0, 1, 3, 2)]
 
     barrier = pltpu.get_barrier_semaphore()
     for peer in peers:
-        pl.semaphore_signal(barrier, inc=1, device_id=(peer, zb), device_id_type=MESH)
+
+        @pl.when(peer != ya)
+        def _():
+            pl.semaphore_signal(barrier, inc=1, device_id=(peer, zb), device_id_type=MESH)
+
     for d in (1, 3, 2):
         pl.semaphore_signal(barrier, inc=1, device_id=(ya, (zb + d) & 3), device_id_type=MESH)
-    for y in range(16):
+    for y in range(4, 16):
         load(y).start()
-    for t in tables[1:]:
-        t.start()
 
     def a_slot(c, who):
         return a_in.at[pl.ds(pl.multiple_of(c * 512 + who * 16, 16), 16)]
@@ -90,14 +96,17 @@
     def send_a(c):
         pltpu.make_async_copy(a_source(c, ya), a_slot(c, ya), a_recv.at[c]).start()
         for peer in peers:
-            pltpu.make_async_remote_copy(
-                src_ref=a_source(c, peer),
-                dst_ref=a_slot(c, ya),
-                send_sem=a_send,
-                recv_sem=a_recv.at[c],
-                device_id=(peer, zb),
-                device_id_type=MESH,
-            ).start()
+
+            @pl.when(peer != ya)
+            def _():
+                pltpu.make_async_remote_copy(
+                    src_ref=a_source(c, peer),
+                    dst_ref=a_slot(c, ya),
+                    send_sem=a_send,
+                    recv_sem=a_recv.at[c],
+                    device_id=(peer, zb),
+                    device_id_type=MESH,
+                ).start()
 
     @scoped
     def wait_a(c):
@@ -148,25 +157,28 @@
 
     rows = 32 * EARLY
     with jax.named_scope("early"):
-        for g in range(4):
+        for g, (y0, ny) in enumerate(GROUPS):
             bhs, bls = [], []
-            landed = xin.at[pl.ds(4 * g, 4)]
-            with jax.named_scope(f'ld{g}'):
+            landed = xin.at[pl.ds(y0, ny)]
+            with jax.named_scope(f"ld{g}"):
                 pltpu.make_async_copy(landed, landed, load_sem.at[g]).wait()
-            for y in range(4 * g, 4 * g + 4):
+            for y in range(y0, y0 + ny):
                 high, low = split(xin[y])
                 xh[y] = high
                 xl[y] = low
                 bhs.append(high)
                 bls.append(low)
+            if g == 2:
+                for t in tables[1:]:
+                    t.start()
             if g == 0:
-                with jax.named_scope('tab'):
+                with jax.named_scope("tab"):
                     tables[0].wait()
             bh, bl = jnp.concatenate(bhs, axis=1), jnp.concatenate(bls, axis=1)
             both = dot(h1[...], bh)
             r = both[:rows] + (both[rows:] + dot(h1[pl.ds(0, rows), :], bl))
-            for k in range(4):
-                a_early[pl.ds(4 * g + k, rows, stride=16), :] = r[:, 128 * k : 128 * k + 128]
+            for k in range(ny):
+                a_early[pl.ds(y0 + k, rows, stride=16), :] = r[:, 128 * k : 128 * k + 128]
     with jax.named_scope("barrier_wait"):
         pl.semaphore_wait(barrier, 34)
     for c in range(EARLY):
@@ -246,7 +258,7 @@
             pltpu.SMEM((512,), f32),
             pltpu.VMEM((4, 128), f32),
             pltpu.VMEM((4, 128), f32),
-            pltpu.SemaphoreType.DMA((4,)),
+            pltpu.SemaphoreType.DMA((len(GROUPS),)),
             pltpu.SemaphoreType.DMA((6,)),
             pltpu.SemaphoreType.DMA,
             pltpu.SemaphoreType.DMA((16,)),

time: 65.3 us -> 64.3 us (0.985)
  Pallas kernels: 63 us -> 61.9 us
    pallas_call x1, Pallas kernels: 63 us -> 61.9 us  [body(): pl.pallas_call(kernel, out_shape=pltpu.VMEM((16, 128, 512), f32), in_spec...]
where the time goes in v2:
time: 64.3 us; the launch traced here: 63.9 us
  Pallas kernels  61.9 us (96%)
  local copies, waits for them, and re-layouts  2.02 us (3%)
    pallas_call x1, Pallas kernels, body(): pl.pallas_call(kernel, out_shape=pltpu.VMEM((16, 128, 512), f32), in_spec...  61.9 us
    unnamed x1, local copies, waits for them, and re-layouts  2.02 us

profile of v2, /device:TPU:1, one launch (start us, length us, event | category | flops | bytes accessed | tf_op | source)
XLA Modules:
  0.0 63.9 jit_solution(5228925770077934302)
XLA Ops:
  0.0 61.9 %shard_map.73 = f32[16,128,512]{2,1,0:T(8,128)S(1)} custom-call(f32[512,16,1,128]{3,2,1,0:T(1,128)} %bitcast.3, bf16[128,512]{1,0:T(8,128)(2,1)} %constant.6.clone.h1_hbm, bf16[512,512]{1,0:T(8,128)(2,1)} %constant.7.clone.hh_hbm, bf16[512,512]{1,0:T(8,128)(2,1)} %constant.8.clone.hl_hbm, f32[512]{0:T(512)} %sx_hbm.1, f32[4,128]{1,0:T(4,128)} %bitcast.4, ...), custom_call_target="tpu_custom_call" | custom-call | tf_op jit(solution)/shard_map/pallas_call | solution.py:240
  61.9 2.0 %copy.9 = f32[16,128,512]{2,1,0:T(8,128)} copy(f32[16,128,512]{2,1,0:T(8,128)S(1)} %shard_map.73) | data formatting | bytes 8388608

commit v3 on v2

--- a/solution.py
+++ b/solution.py
@@ -25,6 +25,7 @@
 YPARTS = ((1, 3), (2, 0))
 AHEAD = 3
 LAG = 2
+FINAL = 1
 GROUPS = ((0, 4), (4, 4), (8, 4), (12, 4))
 
 
@@ -49,8 +50,8 @@
 
 
 def kernel(
-    src, h1_hbm, hh_hbm, hl_hbm, sx_hbm, sy_hbm, sz_hbm, out,
-    xin, xh, xl, h1, hh, hl, a_early, a_out, a_in, b_out, b_in, ycol, sx, sy, sz,
+    src, h1_hbm, hh_hbm, hl_hbm, sx_hbm, sy_hbm, sz_hbm, out, b_in, hh, hl,
+    xin, xh, xl, h1, a_early, a_out, a_in, b_out, ycol, sx, sy, sz,
     load_sem, table_sem, a_send, a_recv, b_send, b_recv,
 ):
     ya, zb = lax.axis_index("ya"), lax.axis_index("zb")
@@ -117,16 +118,16 @@
     def transform_y(c):
         bh, bl = split(a_in[pl.ds(pl.multiple_of(c * 512, 512), 512), :])
         rhs = jnp.concatenate([bh, bh, bl], axis=0)
-        for ds in YPARTS:
-            blocks = [(zb + d) & 3 for d in ds]
-            rows = [pl.ds(pl.multiple_of(b * 128, 128), 128) for b in blocks]
+        for blocks in ((0, 1), (3, 2)):
+            rows = [slice(128 * b, 128 * b + 128) for b in blocks]
             high = jnp.concatenate([hh[r, :] for r in rows], axis=0)
             low = jnp.concatenate([hl[r, :] for r in rows], axis=0)
             r = dot(jnp.concatenate([high, low, high], axis=1), rhs)
-            for i, (d, b) in enumerate(zip(ds, blocks)):
-                target = b_out if d else b_in
-                target[c * 4 + b] = r[128 * i : 128 * i + 128, :]
-                if d:
+            for i, b in enumerate(blocks):
+                b_out[c * 4 + b] = r[128 * i : 128 * i + 128, :]
+
+                @pl.when(zb != b)
+                def _():
                     pltpu.make_async_remote_copy(
                         src_ref=b_out.at[c * 4 + b],
                         dst_ref=b_in.at[c * 4 + zb],
@@ -136,9 +137,13 @@
                         device_id_type=MESH,
                     ).start()
 
+                @pl.when(zb == b)
+                def _():
+                    pltpu.make_async_copy(b_out.at[c * 4 + b], b_in.at[c * 4 + b], b_recv.at[c]).start()
+
     @scoped
     def wait_b(c):
-        slots = b_in.at[pl.ds(c * 4, 3)]
+        slots = b_in.at[pl.ds(c * 4, 4)]
         pltpu.make_async_copy(slots, slots, b_recv.at[c]).wait()
 
     @scoped
@@ -221,7 +226,10 @@
     @pl.loop(16 - LAG, 16)
     def _(c):
         wait_b(c)
-        transform_z(c)
+
+        @pl.when(c < 15)
+        def _():
+            transform_z(c)
 
     with jax.named_scope("drain"):
 
@@ -229,6 +237,33 @@
         pltpu.make_async_copy(sent, sent, a_send).wait()
         sent = b_out.at[pl.ds(0, 16 * 3)]
         pltpu.make_async_copy(sent, sent, b_send).wait()
+
+
+def finish(done, b_in, hh, hl, sx_hbm, sy_hbm, sz_hbm, out, last, sx, sy, sz, out_sem, sem):
+    ya, zb = lax.axis_index("ya"), lax.axis_index("zb")
+    loads = [pltpu.make_async_copy(s, d, sem.at[k]) for k, (s, d) in enumerate(((sx_hbm, sx), (sy_hbm, sy), (sz_hbm, sz)))]
+    for t in loads:
+        t.start()
+    first = 16 - FINAL
+    pltpu.make_async_copy(done.at[pl.ds(0, first)], out.at[pl.ds(0, first)], out_sem).start()
+    for t in loads:
+        t.wait()
+    ycol = jnp.transpose(jnp.broadcast_to(sy[pl.ds(zb, 1), :], (128, 128)))
+    for i in range(FINAL):
+        c = first + i
+        ah, al = split(jnp.concatenate([b_in[c * 4 + b] for b in range(4)], axis=1))
+        lhs = jnp.concatenate([ah, ah, al], axis=1)
+        column = ycol + sx[ya * 16 + c]
+        for k in range(2):
+            cols = slice(256 * k, 256 * k + 256)
+            rhs = jnp.concatenate([hh[:, cols], hl[:, cols], hh[:, cols]], axis=0)
+            r = dot(lhs, rhs)
+            for j in range(2):
+                n = 2 * k + j
+                scale = lax.rsqrt(column + sz[pl.ds(n, 1), :])
+                last[i, :, 128 * n : 128 * n + 128] = r[:, 128 * j : 128 * j + 128] * scale
+        pltpu.make_async_copy(last.at[i], out.at[c], out_sem).start()
+    pltpu.make_async_copy(out, out, out_sem).wait()
 
 
 def body(source, symbol_x, symbol_y, symbol_z):
@@ -237,22 +272,24 @@
     stacked = np.concatenate([high[order], low[order]])
     any_space = pl.BlockSpec(memory_space=pl.ANY)
     f32, bf16 = jnp.float32, jnp.bfloat16
-    return pl.pallas_call(
+    done, b_in, hh, hl = pl.pallas_call(
         kernel,
-        out_shape=pltpu.VMEM((16, 128, 512), f32),
+        out_shape=(
+            pltpu.VMEM((16, 128, 512), f32),
+            pltpu.VMEM((64, 128, 128), f32),
+            pltpu.VMEM((512, 512), bf16),
+            pltpu.VMEM((512, 512), bf16),
+        ),
         in_specs=[any_space] * 7,
-        out_specs=pl.BlockSpec(memory_space=pltpu.VMEM),
+        out_specs=(pl.BlockSpec(memory_space=pltpu.VMEM),) * 4,
         scratch_shapes=[
             pltpu.VMEM((16, 512, 128), f32),
             pltpu.VMEM((16, 512, 128), bf16),
             pltpu.VMEM((16, 512, 128), bf16),
             pltpu.VMEM(stacked.shape, bf16),
-            pltpu.VMEM((512, 512), bf16),
-            pltpu.VMEM((512, 512), bf16),
             pltpu.VMEM((len(order) * 16, 128), f32),
             pltpu.VMEM((8192, 128), f32),
             pltpu.VMEM((8192, 128), f32),
-            pltpu.VMEM((64, 128, 128), f32),
             pltpu.VMEM((64, 128, 128), f32),
             pltpu.VMEM((128, 128), f32),
             pltpu.SMEM((512,), f32),
@@ -266,7 +303,7 @@
             pltpu.SemaphoreType.DMA((16,)),
         ],
         compiler_params=pltpu.CompilerParams(
-            collective_id=0, has_side_effects=True, vmem_limit_bytes=67043328 - 4 * 1024 * 1024 - 65536
+            collective_id=0, has_side_effects=True, vmem_limit_bytes=67043328 - 9 * 1024 * 1024 - 65536
         ),
     )(
         source.reshape(512, 16, 1, 128),
@@ -277,6 +314,21 @@
         symbol_y.reshape(4, 128),
         symbol_z.reshape(4, 128),
     )
+    return pl.pallas_call(
+        finish,
+        out_shape=jax.ShapeDtypeStruct((16, 128, 512), f32),
+        in_specs=[pl.BlockSpec(memory_space=pltpu.VMEM)] * 4 + [any_space] * 3,
+        out_specs=any_space,
+        scratch_shapes=[
+            pltpu.VMEM((FINAL, 128, 512), f32),
+            pltpu.SMEM((512,), f32),
+            pltpu.VMEM((4, 128), f32),
+            pltpu.VMEM((4, 128), f32),
+            pltpu.SemaphoreType.DMA,
+            pltpu.SemaphoreType.DMA((3,)),
+        ],
+        compiler_params=pltpu.CompilerParams(vmem_limit_bytes=32 * 1024 * 1024),
+    )(done, b_in, hh, hl, symbol_x, symbol_y.reshape(4, 128), symbol_z.reshape(4, 128))
 
 
 def solution(mesh):

time: 64.3 us -> 64.1 us (level)
  local copies, waits for them, and re-layouts: 2.02 us -> 0.01 us
  Pallas kernels: 61.9 us -> 63.9 us
    pallas_call x1 -> x2, Pallas kernels: 61.9 us -> 63.9 us  [the longest x1 61.9 us: body(): pl.pallas_call(kernel, out_shape=(pltpu.VMEM((16, 128, 512), f32), pltpu....]
    unnamed x1 -> x6, local copies, waits for them, and re-layouts: 2.02 us -> 0.01 us
where the time goes in v3:
time: 64.1 us; the launch traced here: 64 us
  Pallas kernels  63.9 us (100%)
    pallas_call x1, Pallas kernels, body(): pl.pallas_call(kernel, out_shape=(pltpu.VMEM((16, 128, 512), f32), pltpu....  61.9 us
    pallas_call x1, Pallas kernels, body(): pl.pallas_call(finish, out_shape=jax.ShapeDtypeStruct((16, 128, 512), f32...  2.04 us

profile of v3, /device:TPU:1, one launch (start us, length us, event | category | flops | bytes accessed | tf_op | source)
XLA Modules:
  0.0 64.0 jit_solution(11793426425796524581)
XLA Ops:
  0.0 0.0 copy-start
  0.0 0.0 copy-start.2
  0.0 0.0 copy-start.1
  0.0 61.9 %shard_map.73 = (f32[16,128,512]{2,1,0:T(8,128)S(1)}, f32[64,128,128]{2,1,0:T(8,128)S(1)}, bf16[512,512]{1,0:T(8,128)(2,1)S(1)}, bf16[512,512]{1,0:T(8,128)(2,1)S(1)}) custom-call(f32[512,16,1,128]{3,2,1,0:T(1,128)} %bitcast.7, bf16[128,512]{1,0:T(8,128)(2,1)} %constant.6.clone.h1_hbm, bf16[512,512]{1,0:T(8,128)(2,1)} %constant.7.clone.hh_hbm, ...), custom_call_target="tpu_custom_call" | custom-call | tf_op jit(solution)/shard_map/pallas_call | solution.py:275
  61.9 0.0 copy-done
  61.9 0.0 copy-done.2
  61.9 0.0 copy-done.1
  61.9 2.0 %shard_map.74 = f32[16,128,512]{2,1,0:T(8,128)} custom-call(f32[16,128,512]{2,1,0:T(8,128)S(1)} %get-tuple-element.9.done, f32[64,128,128]{2,1,0:T(8,128)S(1)} %get-tuple-element.10.b_in, bf16[512,512]{1,0:T(8,128)(2,1)S(1)} %get-tuple-element.11.hh, bf16[512,512]{1,0:T(8,128)(2,1)S(1)} %get-tuple-element.12.hl, f32[512]{0:T(512)S(1)} %copy-done, ...), custom_call_target="tpu_custom_call" | custom-call | tf_op jit(solution)/shard_map/pallas_call | solution.py:317
Async XLA Ops:
  0.0 61.9 %copy-start = (f32[512]{0:T(512)S(1)}, f32[512]{0:T(512)}, u32[]{:S(2)}) copy-start(f32[512]{0:T(512)} %sx_hbm.3) | copy-start | bytes 6148
  0.0 61.9 %copy-start.2 = (f32[512]{0:T(512)S(1)}, f32[512]{0:T(512)}, u32[]{:S(2)}) copy-start(f32[512]{0:T(512)} %param.10) | copy-start | bytes 6148
  0.0 61.9 %copy-start.1 = (f32[512]{0:T(512)S(1)}, f32[512]{0:T(512)}, u32[]{:S(2)}) copy-start(f32[512]{0:T(512)} %param.9) | copy-start | bytes 6148

commit v4 on v3

--- a/solution.py
+++ b/solution.py
@@ -186,13 +186,12 @@
                 a_early[pl.ds(y0 + k, rows, stride=16), :] = r[:, 128 * k : 128 * k + 128]
     with jax.named_scope("barrier_wait"):
         pl.semaphore_wait(barrier, 34)
-    for c in range(EARLY):
-        send_a(c)
+    send_a(0)
     for t in tables[1:]:
         t.wait()
     with jax.named_scope("rest"):
 
-        @pl.loop(0, 8, unroll=4)
+        @pl.loop(0, 2, unroll=2)
         def _(g):
             bh = jnp.concatenate([xh[2 * g + k] for k in range(2)], axis=1)
             bl = jnp.concatenate([xl[2 * g + k] for k in range(2)], axis=1)
@@ -203,6 +202,19 @@
                 for k in range(2):
                     a_out[pl.ds(512 * 16 * p + 2 * g + k, 512, stride=16), :] = r[:, 128 * k : 128 * k + 128]
 
+        send_a(1)
+
+        @pl.loop(2, 8, unroll=3)
+        def _(g):
+            bh = jnp.concatenate([xh[2 * g + k] for k in range(2)], axis=1)
+            bl = jnp.concatenate([xl[2 * g + k] for k in range(2)], axis=1)
+            rhs = jnp.concatenate([bh, bh, bl], axis=0)
+            for p in range(1):
+                rows = slice(512 * p, 512 * p + 512)
+                r = dot(jnp.concatenate([hh[rows, :], hl[rows, :], hh[rows, :]], axis=1), rhs)
+                for k in range(2):
+                    a_out[pl.ds(512 * 16 * p + 2 * g + k, 512, stride=16), :] = r[:, 128 * k : 128 * k + 128]
+
     @pl.loop(EARLY, AHEAD)
     def _(c):
         send_a(c)
@@ -245,7 +257,8 @@
     for t in loads:
         t.start()
     first = 16 - FINAL
-    pltpu.make_async_copy(done.at[pl.ds(0, first)], out.at[pl.ds(0, first)], out_sem).start()
+    for k in range(5):
+        pltpu.make_async_copy(done.at[pl.ds(3 * k, 3)], out.at[pl.ds(3 * k, 3)], out_sem).start()
     for t in loads:
         t.wait()
     ycol = jnp.transpose(jnp.broadcast_to(sy[pl.ds(zb, 1), :], (128, 128)))

time: 64.1 us -> 64 us (level)
  no operation moved by 1% of the time
where the time goes in v4:
time: 64 us; the launch traced here: 63.9 us
  Pallas kernels  63.8 us (100%)
    pallas_call x1, Pallas kernels, body(): pl.pallas_call(kernel, out_shape=(pltpu.VMEM((16, 128, 512), f32), pltpu....  61.8 us
    pallas_call x1, Pallas kernels, body(): pl.pallas_call(finish, out_shape=jax.ShapeDtypeStruct((16, 128, 512), f32...  2.04 us

profile of v4, /device:TPU:1, one launch (start us, length us, event | category | flops | bytes accessed | tf_op | source)
XLA Modules:
  0.0 63.9 jit_solution(10933473877958521490)
XLA Ops:
  0.0 0.0 copy-start
  0.0 0.0 copy-start.2
  0.0 0.0 copy-start.1
  0.0 61.8 %shard_map.73 = (f32[16,128,512]{2,1,0:T(8,128)S(1)}, f32[64,128,128]{2,1,0:T(8,128)S(1)}, bf16[512,512]{1,0:T(8,128)(2,1)S(1)}, bf16[512,512]{1,0:T(8,128)(2,1)S(1)}) custom-call(f32[512,16,1,128]{3,2,1,0:T(1,128)} %bitcast.7, bf16[128,512]{1,0:T(8,128)(2,1)} %constant.6.clone.h1_hbm, bf16[512,512]{1,0:T(8,128)(2,1)} %constant.7.clone.hh_hbm, ...), custom_call_target="tpu_custom_call" | custom-call | tf_op jit(solution)/shard_map/pallas_call | solution.py:288
  61.8 0.0 copy-done
  61.8 0.0 copy-done.2
  61.8 0.0 copy-done.1
  61.8 2.0 %shard_map.74 = f32[16,128,512]{2,1,0:T(8,128)} custom-call(f32[16,128,512]{2,1,0:T(8,128)S(1)} %get-tuple-element.9.done, f32[64,128,128]{2,1,0:T(8,128)S(1)} %get-tuple-element.10.b_in, bf16[512,512]{1,0:T(8,128)(2,1)S(1)} %get-tuple-element.11.hh, bf16[512,512]{1,0:T(8,128)(2,1)S(1)} %get-tuple-element.12.hl, f32[512]{0:T(512)S(1)} %copy-done, ...), custom_call_target="tpu_custom_call" | custom-call | tf_op jit(solution)/shard_map/pallas_call | solution.py:330
Async XLA Ops:
  0.0 61.8 %copy-start = (f32[512]{0:T(512)S(1)}, f32[512]{0:T(512)}, u32[]{:S(2)}) copy-start(f32[512]{0:T(512)} %sx_hbm.3) | copy-start | bytes 6148
  0.0 61.8 %copy-start.2 = (f32[512]{0:T(512)S(1)}, f32[512]{0:T(512)}, u32[]{:S(2)}) copy-start(f32[512]{0:T(512)} %param.10) | copy-start | bytes 6148
  0.0 61.8 %copy-start.1 = (f32[512]{0:T(512)S(1)}, f32[512]{0:T(512)}, u32[]{:S(2)}) copy-start(f32[512]{0:T(512)} %param.9) | copy-start | bytes 6148

commit v5 on v4

--- a/solution.py
+++ b/solution.py
@@ -95,7 +95,7 @@
 
     @scoped
     def send_a(c):
-        pltpu.make_async_copy(a_source(c, ya), a_slot(c, ya), a_recv.at[c]).start()
+        pltpu.make_async_copy(a_source(c, ya), a_slot(c, ya), a_recv.at[c % 8]).start()
         for peer in peers:
 
             @pl.when(peer != ya)
@@ -104,7 +104,7 @@
                     src_ref=a_source(c, peer),
                     dst_ref=a_slot(c, ya),
                     send_sem=a_send,
-                    recv_sem=a_recv.at[c],
+                    recv_sem=a_recv.at[c % 8],
                     device_id=(peer, zb),
                     device_id_type=MESH,
                 ).start()
@@ -112,7 +112,7 @@
     @scoped
     def wait_a(c):
         slots = a_in.at[pl.ds(pl.multiple_of(c * 512, 512), 512)]
-        pltpu.make_async_copy(slots, slots, a_recv.at[c]).wait()
+        pltpu.make_async_copy(slots, slots, a_recv.at[c % 8]).wait()
 
     @scoped
     def transform_y(c):
@@ -132,19 +132,19 @@
                         src_ref=b_out.at[c * 4 + b],
                         dst_ref=b_in.at[c * 4 + zb],
                         send_sem=b_send,
-                        recv_sem=b_recv.at[c],
+                        recv_sem=b_recv.at[c % 8],
                         device_id=(ya, b),
                         device_id_type=MESH,
                     ).start()
 
                 @pl.when(zb == b)
                 def _():
-                    pltpu.make_async_copy(b_out.at[c * 4 + b], b_in.at[c * 4 + b], b_recv.at[c]).start()
+                    pltpu.make_async_copy(b_out.at[c * 4 + b], b_in.at[c * 4 + b], b_recv.at[c % 8]).start()
 
     @scoped
     def wait_b(c):
         slots = b_in.at[pl.ds(c * 4, 4)]
-        pltpu.make_async_copy(slots, slots, b_recv.at[c]).wait()
+        pltpu.make_async_copy(slots, slots, b_recv.at[c % 8]).wait()
 
     @scoped
     def transform_z(c):
@@ -311,9 +311,9 @@
             pltpu.SemaphoreType.DMA((len(GROUPS),)),
             pltpu.SemaphoreType.DMA((6,)),
             pltpu.SemaphoreType.DMA,
-            pltpu.SemaphoreType.DMA((16,)),
+            pltpu.SemaphoreType.DMA((8,)),
             pltpu.SemaphoreType.DMA,
-            pltpu.SemaphoreType.DMA((16,)),
+            pltpu.SemaphoreType.DMA((8,)),
         ],
         compiler_params=pltpu.CompilerParams(
             collective_id=0, has_side_effects=True, vmem_limit_bytes=67043328 - 9 * 1024 * 1024 - 65536

time: 64 us -> 63.8 us (level)
  no operation moved by 1% of the time
where the time goes in v5:
time: 63.8 us; the launch traced here: 63.7 us
  Pallas kernels  63.7 us (100%)
    pallas_call x1, Pallas kernels, body(): pl.pallas_call(kernel, out_shape=(pltpu.VMEM((16, 128, 512), f32), pltpu....  61.6 us
    pallas_call x1, Pallas kernels, body(): pl.pallas_call(finish, out_shape=jax.ShapeDtypeStruct((16, 128, 512), f32...  2.04 us

profile of v5, /device:TPU:1, one launch (start us, length us, event | category | flops | bytes accessed | tf_op | source)
XLA Modules:
  0.0 63.7 jit_solution(2506015761043548134)
XLA Ops:
  0.0 0.0 copy-start
  0.0 0.0 copy-start.2
  0.0 0.0 copy-start.1
  0.0 61.6 %shard_map.73 = (f32[16,128,512]{2,1,0:T(8,128)S(1)}, f32[64,128,128]{2,1,0:T(8,128)S(1)}, bf16[512,512]{1,0:T(8,128)(2,1)S(1)}, bf16[512,512]{1,0:T(8,128)(2,1)S(1)}) custom-call(f32[512,16,1,128]{3,2,1,0:T(1,128)} %bitcast.7, bf16[128,512]{1,0:T(8,128)(2,1)} %constant.6.clone.h1_hbm, bf16[512,512]{1,0:T(8,128)(2,1)} %constant.7.clone.hh_hbm, ...), custom_call_target="tpu_custom_call" | custom-call | tf_op jit(solution)/shard_map/pallas_call | solution.py:288
  61.6 0.0 copy-done
  61.6 0.0 copy-done.2
  61.7 0.0 copy-done.1
  61.7 2.0 %shard_map.74 = f32[16,128,512]{2,1,0:T(8,128)} custom-call(f32[16,128,512]{2,1,0:T(8,128)S(1)} %get-tuple-element.9.done, f32[64,128,128]{2,1,0:T(8,128)S(1)} %get-tuple-element.10.b_in, bf16[512,512]{1,0:T(8,128)(2,1)S(1)} %get-tuple-element.11.hh, bf16[512,512]{1,0:T(8,128)(2,1)S(1)} %get-tuple-element.12.hl, f32[512]{0:T(512)S(1)} %copy-done, ...), custom_call_target="tpu_custom_call" | custom-call | tf_op jit(solution)/shard_map/pallas_call | solution.py:330
Async XLA Ops:
  0.0 61.6 %copy-start = (f32[512]{0:T(512)S(1)}, f32[512]{0:T(512)}, u32[]{:S(2)}) copy-start(f32[512]{0:T(512)} %sx_hbm.3) | copy-start | bytes 6148
  0.0 61.6 %copy-start.2 = (f32[512]{0:T(512)S(1)}, f32[512]{0:T(512)}, u32[]{:S(2)}) copy-start(f32[512]{0:T(512)} %param.10) | copy-start | bytes 6148
  0.0 61.7 %copy-start.1 = (f32[512]{0:T(512)S(1)}, f32[512]{0:T(512)}, u32[]{:S(2)}) copy-start(f32[512]{0:T(512)} %param.9) | copy-start | bytes 6148
